TPU v7x, 256 devices: a whole 4x4x8 slice. The times are simulated.
256 devices in a mesh: mp: 64 (over z, x, core), head: 4 (over y).
Axes of the slice: x: 4, y: 4, z: 8, core: 2. Of those that a mesh axis runs over, the one named last changes fastest.
Arguments:
- hidden: bfloat16 [8, 4096], replicated, may hold values from -6 to 6
- norm_gain: float32 [4096], replicated, may hold values from 0.25 to 1.75
- w_query: bfloat16 [4096, 4096], P('mp', 'head'), may hold values from -0.09375 to 0.09375
- enc_states: bfloat16 [8, 4096, 4096], P(None, 'mp'), may hold values from -6 to 6
- w_key: bfloat16 [4096, 4096], P('mp', 'head'), may hold values from -0.09375 to 0.09375
- w_value: bfloat16 [4096, 4096], P('mp', 'head'), may hold values from -0.09375 to 0.09375
- w_out: bfloat16 [4096, 4096], P('head', 'mp'), may hold values from -0.09375 to 0.09375
- bias_table: float32 [32, 64], P(None, 'head'), may hold values from -5 to 300
- buckets: int32 [8, 4096], P(None, 'mp'), may hold values from 0 to 31
- src_len: int32 [8], replicated, may hold values from 512 to 4096
Outputs:
- updated: bfloat16 [8, 4096], P(None, 'mp')
All inputs are finite; a program needn't handle non-finite values.
Results may differ from a plain program's by a relative error of at most 0.0049.
Values may be sent and summed in bfloat16 or wider, within the bound.
A program may use at most 128 MiB of HBM per device.

v0:
```python
import jax
import jax.numpy as jnp
from jax import lax
from jax.sharding import Mesh
from jax.sharding import PartitionSpec as P

MP = ("mp_0", "mp_1", "mp_2")


EPSILON = 1e-06
NEGATIVE = -1e30


def sent_together(arrays, axis, dim, along):
    widths = [a.shape[along] for a in arrays]
    both = jnp.concatenate(arrays, axis=along)
    filled = lax.all_gather(both, axis, axis=dim, tiled=True)
    return tuple(jnp.split(filled, [sum(widths[:k]) for k in range(1, len(widths))], axis=along))


def all_in_one(array, axis):
    leaves = jax.tree.leaves(array)
    order = sorted(range(len(leaves)), key=lambda k: -leaves[k].size)
    width = (1, *leaves[order[0]].shape)[-1]
    lines = [
        jnp.pad(leaves[k].reshape(-1), (0, -leaves[k].size % width)).reshape(-1, width)
        for k in order
    ]
    both, at, found = (lax.all_gather(jnp.concatenate(lines), axis), 0, {})
    for k, line in zip(order, lines):
        piece = both[:, at : at + len(line)].reshape(len(both), -1)
        found[k] = piece[:, : leaves[k].size].reshape(-1, *leaves[k].shape)
        at += len(line)
    numbers = iter(range(len(leaves)))
    return jax.tree.map(lambda _: found[next(numbers)], array)


def joined_all(array, axes, combine):
    for axis in axes:
        pieces = all_in_one(array, axis)
        array = jax.tree.map(lambda part: part[0], pieces)
        for k in range(1, lax.axis_size(axis)):
            array = combine(array, jax.tree.map(lambda part: part[k], pieces))
    return array


def copy_for_each(array, axis):
    copies = jnp.broadcast_to(array, (lax.axis_size(axis), *array.shape))
    return lax.all_to_all(copies, axis, split_axis=0, concat_axis=0, tiled=True)


def taken_together(array, axis):
    return copy_for_each(array, axis).sum(axis=0)


def add_columns(source, weights):
    return jnp.dot(source, weights, preferred_element_type=jnp.float32)


def combine_parts(first, second):
    merged_max = jnp.maximum(first[0], second[0])
    first_scale = jnp.exp(first[0] - merged_max)
    second_scale = jnp.exp(second[0] - merged_max)
    denominator = first[1] * first_scale + second[1] * second_scale
    weighted = first[2] * first_scale[:, :, None] + second[2] * second_scale[:, :, None]
    return (merged_max, denominator, weighted)


def shards(
    hidden, norm_gain, w_query, enc_states, w_key, w_value, w_out, bias_table, buckets, src_len
):
    batch_size, src_local, model_width = enc_states.shape
    local_inner = w_key.shape[1]
    local_heads = bias_table.shape[1]
    head_size = local_inner // local_heads
    my_index = lax.axis_index(MP)
    widened = hidden.astype(jnp.float32)
    mean_square = jnp.mean(widened * widened, axis=-1, keepdims=True)
    normed = (widened * lax.rsqrt(mean_square + EPSILON) * norm_gain).astype(jnp.bfloat16)
    factor = float(head_size) ** (-0.5)
    enc_rows = enc_states.reshape(batch_size * src_local, model_width)
    blocks = sent_together((w_query, w_key, w_value), MP, 0, 1)
    query_sum = add_columns(normed, blocks[0])
    key_sum = add_columns(enc_rows, blocks[1])
    value_sum = add_columns(enc_rows, blocks[2])
    query = query_sum.astype(jnp.bfloat16).reshape(batch_size, local_heads, head_size)
    key_rows = key_sum.reshape(batch_size, src_local, local_heads, head_size)
    value_rows = value_sum.reshape(batch_size, src_local, local_heads, head_size)
    scores = (
        jnp.einsum(
            "bhd,bshd->bhs", query.astype(jnp.float32), key_rows, precision=lax.Precision.HIGHEST
        )
        * factor
    )
    bucket_ids = jnp.arange(bias_table.shape[0], dtype=jnp.int32)
    one_hot = (buckets[:, :, None] == bucket_ids[None, None, :]).astype(jnp.float32)
    scores = scores + jnp.einsum(
        "bsk,kh->bhs", one_hot, bias_table, precision=lax.Precision.HIGHEST
    )
    positions = my_index * src_local + jnp.arange(src_local, dtype=jnp.int32)
    is_live = (positions[None, :] < src_len[:, None])[:, None, :]
    scores = jnp.where(is_live, scores, NEGATIVE)
    local_max = jnp.max(scores, axis=-1)
    weights = jnp.where(is_live, jnp.exp(scores - local_max[:, :, None]), 0.0)
    denominator = jnp.sum(weights, axis=-1)
    weighted = jnp.einsum("bhs,bshd->bhd", weights, value_rows, precision=lax.Precision.HIGHEST)
    best_max, denominator, weighted = joined_all(
        (local_max, denominator, weighted), MP, combine_parts
    )
    context = (
        (weighted / denominator[:, :, None]).reshape(batch_size, local_inner).astype(jnp.bfloat16)
    )
    partial_value = jnp.dot(context, w_out, preferred_element_type=jnp.float32)
    summed = taken_together(partial_value, "head")
    out_cols = w_out.shape[1]
    residual = lax.dynamic_slice_in_dim(widened, my_index * out_cols, out_cols, 1)
    return (summed + residual).astype(jnp.bfloat16)


def solution(mesh):
    finer = Mesh(
        mesh.devices.reshape(8, 4, 2, mesh.shape["head"]), ("mp_0", "mp_1", "mp_2", "head")
    )
    in_specs = (
        P(),
        P(),
        P(MP, "head"),
        P(None, MP, None),
        P(MP, "head"),
        P(MP, "head"),
        P("head", MP),
        P(None, "head"),
        P(None, MP),
        P(),
    )
    out_specs = P(None, MP)
    return jax.shard_map(
        shards, mesh=finer, in_specs=in_specs, out_specs=out_specs, check_vma=False
    )
```

profile of v0, /device:TPU:1, one launch (start us, length us, event | category | flops | bytes accessed | tf_op | source)
XLA Modules:
  0.0 237.7 jit_solution(2552572958169257879)
XLA Ops:
  6.5 1.9 pad_maximum_fusion
  8.5 1.0 multiply_reduce_fusion
  9.5 0.7 broadcast_compare_fusion
  10.2 124.5 %all-gather.8.cloned.1.call-done = bf16[4096,3072]{1,0:T(8,128)(2,1)} async-done(((bf16[64,3072]{1,0:T(8,128)(2,1)}), bf16[4096,3072]{1,0:T(8,128)(2,1)}) %all-gather.8.cloned.1.call-update) | async-done | bytes 25165840 | tf_op jit(solution)/shard_map/all_gather | solution.py:17
  134.7 4.7 %fusion.18 = bf16[8,1024]{1,0:T(8,128)(2,1)S(1)} fusion(bf16[4096,3072]{1,0:T(8,128)(2,1)} %all-gather.8.cloned.1.call-done, f32[4096]{0:T(1024)} %param.11, f32[8]{0:T(128)S(1)} %add_rsqrt_fusion, bf16[8,4096]{1,0:T(8,128)(2,1)} %param.10), kind=kOutput, calls=%fused_computation.15 | convolution fusion | flops 67248128 | bytes 8486944 | tf_op jit(solution)/shard_map/dot_general | solution.py:57
  139.3 0.1 reshape.694
  139.4 8.3 %fusion.10 = f32[512,1024]{0,1:T(8,128)S(1)} fusion(bf16[512,4096]{1,0:T(8,128)(2,1)} %bitcast.411, bf16[4096,3072]{1,0:T(8,128)(2,1)} %all-gather.8.cloned.1.call-done), kind=kOutput, calls=%fused_computation.10 | convolution fusion | flops 4294967296 | bytes 14680064 | tf_op jit(solution)/shard_map/dot_general | solution.py:57
  147.7 2.4 %reshape.671 = f32[8,64,16,64]{1,0,3,2:T(8,128)} reshape(f32[512,1024]{0,1:T(8,128)S(1)} %fusion.10) | data formatting | bytes 4194304 | tf_op jit(solution)/shard_map/reshape | solution.py:87
  150.2 4.6 %fusion.8 = f32[8,16,1,64]{3,2,1,0:T(1,128)S(1)} fusion(bf16[8,16,64,1]{2,3,1,0:T(2,128)(2,1)S(1)} %reshape.694, f32[8,64,16,64]{1,0,3,2:T(8,128)} %reshape.671), kind=kOutput, calls=%fused_computation.8 | convolution fusion | flops 6291456 | bytes 2146304 | tf_op jit(solution)/shard_map/bhd,bshd->bhs/dot_general | solution.py:90
  154.8 0.3 fusion.112
  155.1 0.2 fusion.107
  155.3 8.3 %fusion.13 = f32[512,1024]{0,1:T(8,128)S(1)} fusion(bf16[512,4096]{1,0:T(8,128)(2,1)} %bitcast.412, bf16[4096,3072]{1,0:T(8,128)(2,1)} %all-gather.8.cloned.1.call-done), kind=kOutput, calls=%fused_computation.11 | convolution fusion | flops 4294967296 | bytes 14680064 | tf_op jit(solution)/shard_map/dot_general | solution.py:57
  163.6 2.4 %reshape.672 = f32[8,64,16,64]{1,0,3,2:T(8,128)} reshape(f32[512,1024]{0,1:T(8,128)S(1)} %fusion.13) | data formatting | bytes 4194304 | tf_op jit(solution)/shard_map/reshape | solution.py:88
  166.0 8.8 %fusion.6 = f32[8,16,1,64]{3,2,1,0:T(1,128)S(1)} fusion(f32[8,16,64,1]{2,3,1,0:T(1,128)S(1)} %bitcast.409, f32[8,64,16,64]{1,0,3,2:T(8,128)} %reshape.672), kind=kOutput, calls=%fused_computation.6 | convolution fusion | flops 6291456 | bytes 2162688 | tf_op jit(solution)/shard_map/bhs,bshd->bhd/dot_general | solution.py:106
  175.0 19.7 %all-gather.3 = f32[8,132,64]{1,2,0:T(8,128)S(1)} all-gather(f32[1,132,64]{1,2,0:T(8,128)S(1)} %copy.106), channel_id=2, replica_groups=mesh['mp_0'=8,'mp_1'=4,'mp_2'=2,'head'=4] {'mp_0'}, dimensions={0}, use_global_device_ids=true | all-gather | bytes 304128 | tf_op jit(solution)/shard_map/all_gather | solution.py:29
  194.7 0.1 fusion.108
  196.9 0.1 copy.131
  196.9 0.1 copy.132
  197.2 9.4 %all-gather.4 = f32[4,132,64]{1,2,0:T(8,128)S(1)} all-gather(f32[1,132,64]{1,2,0:T(8,128)S(1)} %maximum_bitcast_fusion.1), channel_id=3, replica_groups=mesh['mp_0'=8,'mp_1'=4,'mp_2'=2,'head'=4] {'mp_1'}, dimensions={0}, use_global_device_ids=true | all-gather | bytes 168960 | tf_op jit(solution)/shard_map/all_gather | solution.py:29
  207.7 0.1 copy.145
  207.8 0.1 copy.146
  208.0 10.2 %all-gather.5 = f32[2,132,64]{1,2,0:T(8,128)S(1)} all-gather(f32[1,132,64]{1,2,0:T(8,128)S(1)} %maximum_bitcast_fusion.2), channel_id=4, replica_groups=mesh['mp_0'=8,'mp_1'=4,'mp_2'=2,'head'=4] {'mp_2'}, dimensions={0}, use_global_device_ids=true | all-gather | bytes 101376 | tf_op jit(solution)/shard_map/all_gather | solution.py:29
  218.9 0.1 copy.147
  219.3 0.1 div.16
  219.4 0.1 mul.402
  219.9 0.1 fusion.55
  220.0 0.7 reshape.695
  220.7 4.0 %all-to-all-start = ((f32[4,1,512]{2,1,0:T(1,128)}), f32[4,1,512]{2,1,0:T(1,128)S(1)}, u32[]{:S(2)}, u32[]{:S(2)}) async-start(f32[4,1,512]{2,1,0:T(1,128)} %reshape.695), calls=%async_computation | async-start | bytes 16384 | tf_op jit(solution)/shard_map/all_to_all | solution.py:49
  224.7 4.2 %all-to-all-done = f32[4,1,512]{2,1,0:T(1,128)S(1)} async-done(((f32[4,1,512]{2,1,0:T(1,128)}), f32[4,1,512]{2,1,0:T(1,128)S(1)}, u32[]{:S(2)}, u32[]{:S(2)}) %all-to-all-start) | async-done | bytes 8224 | tf_op jit(solution)/shard_map/all_to_all | solution.py:49
  228.9 0.5 broadcast.66
  229.4 0.7 reduce
  230.2 0.7 add_convert_fusion
  (87 shorter events, 4.9 us)
Async XLA Ops:
  6.5 213.3 %copy-start = (bf16[1024,64]{0,1:T(8,128)(2,1)S(1)}, bf16[1024,64]{0,1:T(8,128)(2,1)}, u32[]{:S(2)}) copy-start(bf16[1024,64]{0,1:T(8,128)(2,1)} %param.16) | copy-start | bytes 393220
  6.5 128.1 %all-gather.8.cloned.1.call-start = ((), (), s32[]{:S(2)}) async-start(), calls=%async_computation.1 | async-start | bytes 25559040 | tf_op jit(solution)/shard_map/all_gather | solution.py:17
  147.7 7.0 %copy-start.2 = (f32[32,16]{0,1:T(8,128)S(1)}, f32[32,16]{0,1:T(8,128)}, u32[]{:S(2)}) copy-start(f32[32,16]{0,1:T(8,128)} %param.17) | copy-start | bytes 6148
  147.7 7.0 %copy-start.3 = (s32[8,64]{1,0:T(8,128)S(1)}, s32[8,64]{1,0:T(8,128)}, u32[]{:S(2)}) copy-start(s32[8,64]{1,0:T(8,128)} %param.18) | copy-start | bytes 6148
  174.9 49.9 %copy-start.1 = (bf16[8,4096]{1,0:T(8,128)(2,1)S(1)}, bf16[8,4096]{1,0:T(8,128)(2,1)}, u32[]{:S(2)}) copy-start(bf16[8,4096]{1,0:T(8,128)(2,1)} %param.10) | copy-start | bytes 196612
  220.7 8.2 %all-to-all-start = ((f32[4,1,512]{2,1,0:T(1,128)}), f32[4,1,512]{2,1,0:T(1,128)S(1)}, u32[]{:S(2)}, u32[]{:S(2)}) async-start(f32[4,1,512]{2,1,0:T(1,128)} %reshape.695), calls=%async_computation | async-start | bytes 16384 | tf_op jit(solution)/shard_map/all_to_all | solution.py:49
Sparse Core Ops, SparseCore 0:
  10.1 124.5 all-gather.7
where the time goes:
time: 238 us
  waiting for transfers between devices  129 us (54%)
  blocking collectives  39.3 us (17%)
  matrix products  35 us (15%)
  between operations  13.7 us (6%)
  local copies, waits for them, and re-layouts  11.4 us (5%)
  other arithmetic  5.61 us (2%)
  starting transfers between devices  4 us (2%)
    all_gather x1, waiting for transfers between devices, sent_together(): filled = lax.all_gather(both, axis, axis=dim, tiled=True)  124 us
    all_gather x3, blocking collectives, all_in_one(): both, at, found = (lax.all_gather(jnp.concatenate(lines), axis), 0, {})  39.3 us
    dot_general x3, matrix products, add_columns(): return jnp.dot(source, weights, preferred_element_type=jnp.float32)  21.2 us
    dot_general x1, matrix products, shards(): jnp.einsum('bhs,bshd->bhd', weights, value_rows, precision=lax.Precision....  8.84 us
  transfers between devices with their start and end apart: 2, of which 2 were waited for; matrix products, arithmetic and copies ran while one was open for 1% of the time, Pallas kernels for 0%

commit v1 on v0

v1 whole, which is shorter than its diff:
```python
import jax
import jax.numpy as jnp
from jax import lax
from jax.sharding import PartitionSpec as P

EPSILON = 1e-06
NEGATIVE = -1e30


def shards(
    hidden, norm_gain, w_query, enc_states, w_key, w_value, w_out, bias_table, buckets, src_len
):
    batch, src_local, _ = enc_states.shape
    rows, inner = w_key.shape
    heads = bias_table.shape[1]
    head_size = inner // heads
    me = lax.axis_index("mp")
    widened = hidden.astype(jnp.float32)
    mean_square = jnp.mean(widened * widened, axis=-1, keepdims=True)
    normed = (widened * lax.rsqrt(mean_square + EPSILON) * norm_gain).astype(jnp.bfloat16)
    mine = lax.dynamic_slice_in_dim(normed, me * rows, rows, 1)
    query = jnp.dot(mine, w_query, preferred_element_type=jnp.float32)
    query = lax.psum(query, "mp").astype(jnp.bfloat16).reshape(batch, heads, head_size)
    probe = jnp.einsum(
        "bhe,dhe->bhd",
        query,
        w_key.reshape(rows, heads, head_size),
        preferred_element_type=jnp.float32,
    )
    probe = (probe * float(head_size) ** (-0.5)).astype(jnp.bfloat16)
    probe = lax.all_gather(probe, "mp", axis=2, tiled=True)
    scores = jnp.einsum("bhd,bsd->bhs", probe, enc_states, preferred_element_type=jnp.float32)
    ids = jnp.arange(bias_table.shape[0], dtype=jnp.int32)
    one_hot = (buckets[:, :, None] == ids[None, None, :]).astype(jnp.float32)
    scores = scores + jnp.einsum(
        "bsk,kh->bhs", one_hot, bias_table, precision=lax.Precision.HIGHEST
    )
    positions = me * src_local + jnp.arange(src_local, dtype=jnp.int32)
    live = (positions[None, :] < src_len[:, None])[:, None, :]
    scores = jnp.where(live, scores, NEGATIVE)
    top = lax.pmax(jnp.max(scores, axis=-1), "mp")
    weights = jnp.where(live, jnp.exp(scores - top[:, :, None]), 0.0)
    total = lax.psum(jnp.sum(weights, axis=-1), "mp")
    mixed = jnp.einsum(
        "bhs,bsd->bhd",
        weights.astype(jnp.bfloat16),
        enc_states,
        preferred_element_type=jnp.float32,
    )
    mixed = lax.psum_scatter(mixed, "mp", scatter_dimension=2, tiled=True)
    mixed = (mixed / total[:, :, None]).astype(jnp.bfloat16)
    context = jnp.einsum(
        "bhd,dhe->bhe",
        mixed,
        w_value.reshape(rows, heads, head_size),
        preferred_element_type=jnp.float32,
    )
    context = lax.psum(context, "mp").astype(jnp.bfloat16).reshape(batch, inner)
    out = lax.psum(jnp.dot(context, w_out, preferred_element_type=jnp.float32), "head")
    cols = w_out.shape[1]
    residual = lax.dynamic_slice_in_dim(widened, me * cols, cols, 1)
    return (out + residual).astype(jnp.bfloat16)


def solution(mesh):
    in_specs = (
        P(),
        P(),
        P("mp", "head"),
        P(None, "mp", None),
        P("mp", "head"),
        P("mp", "head"),
        P("head", "mp"),
        P(None, "head"),
        P(None, "mp"),
        P(),
    )
    return jax.shard_map(
        shards, mesh=mesh, in_specs=in_specs, out_specs=P(None, "mp"), check_vma=False
    )
```

time: 238 us -> 924 us (3.88)
  blocking collectives: 39.3 us -> 754 us
  waiting for transfers between devices: 129 us -> 91.2 us
  local copies, waits for them, and re-layouts: 11.4 us -> 45 us
  matrix products: 35 us -> 11.3 us
    psum x0 -> x4, blocking collectives: none -> 630 us  [the longest x1 249 us: shards(): lax.psum(query, 'mp').astype(jnp.bfloat16).reshape(batch, heads, head_size)]
    pmax x0 -> x1, blocking collectives: none -> 124 us  [shards(): top = lax.pmax(jnp.max(scores, axis=-1), 'mp')]
    all_gather x1, waiting for transfers between devices: 124 us -> 82.5 us  [shards(): probe = lax.all_gather(probe, 'mp', axis=2, tiled=True)]
    unnamed x11 -> x14, local copies, waits for them, and re-layouts: 0.87 us -> 41.8 us
    all_gather x3 -> x0, blocking collectives: 39.3 us -> none  [all_in_one(): both, at, found = (lax.all_gather(jnp.concatenate(lines), axis), 0, {})]
    dot_general x6, matrix products: 34.8 us -> 11 us  [the longest x1 7.29 us: shards(): jnp.einsum('bhd,bsd->bhs', probe, enc_states, preferred_element_type=jnp....]
  transfers between devices with their start and end apart: 2 -> 2, of which waited for: 2 -> 2; matrix products, arithmetic and copies ran while one was open for 1% -> 0% of each run, Pallas kernels for 0% -> 0%
where the time goes in v1:
time: 924 us; the launch traced here: 918 us
  blocking collectives  754 us (82%)
  waiting for transfers between devices  91.2 us (10%)
  local copies, waits for them, and re-layouts  45 us (5%)
  between operations  13.5 us (1%)
  matrix products  11.3 us (1%)
    psum x1, blocking collectives, shards(): lax.psum(query, 'mp').astype(jnp.bfloat16).reshape(batch, heads, head_size)  249 us
    psum x1, blocking collectives, shards(): context = lax.psum(context, 'mp').astype(jnp.bfloat16).reshape(batch, inner)  246 us
    psum x1, blocking collectives, shards(): total = lax.psum(jnp.sum(weights, axis=-1), 'mp')  126 us
    pmax x1, blocking collectives, shards(): top = lax.pmax(jnp.max(scores, axis=-1), 'mp')  124 us
    all_gather x1, waiting for transfers between devices, shards(): probe = lax.all_gather(probe, 'mp', axis=2, tiled=True)  82.5 us
    unnamed x14, local copies, waits for them, and re-layouts  41.8 us
  transfers between devices with their start and end apart: 2, of which 2 were waited for; matrix products, arithmetic and copies ran while one was open for 0% of the time, Pallas kernels for 0%

profile of v1, /device:TPU:1, one launch (start us, length us, event | category | flops | bytes accessed | tf_op | source)
XLA Modules:
  0.0 918.4 jit_solution(14839864621208806205)
XLA Ops:
  6.5 0.9 convert_element_type.28
  7.4 1.0 multiply_reduce_fusion
  8.4 0.8 dynamic-slice
  9.2 0.2 fusion.19
  9.4 249.4 %psum.28 = bf16[8,1024]{1,0:T(8,128)(2,1)S(1)} all-reduce(f32[8,1024]{1,0:T(8,128)S(1)} %fusion.19), channel_id=1, replica_groups=mesh['mp'=64,'head'=4] {'mp'}, use_global_device_ids=true, to_apply=%region_1.0 | all-reduce | flops 8192 | bytes 49152 | tf_op jit(solution)/shard_map/psum | solution.py:23
  258.8 0.1 reshape.51
  258.9 1.1 reshape.52
  260.0 0.2 fusion.5
  260.3 0.8 copy.16
  261.1 0.0 reduce-scatter.4.cloned.1.call-start
  261.2 0.7 broadcast_compare_fusion
  261.9 82.5 %all-gather.2.cloned.1.call-done = bf16[8,16,4096]{1,0,2:T(8,128)(2,1)} async-done(((bf16[8,16,64]{1,0,2:T(8,128)(2,1)}), bf16[8,16,4096]{1,0,2:T(8,128)(2,1)}) %all-gather.2.cloned.1.call-update) | async-done | bytes 1048592 | tf_op jit(solution)/shard_map/all_gather | solution.py:31
  344.4 7.3 fusion
  351.7 0.3 fusion.24
  352.0 123.7 %pmax.7 = f32[8,16]{1,0:T(8,128)S(1)} all-reduce(f32[8,16]{1,0:T(8,128)S(1)} %get-tuple-element.5), channel_id=1, replica_groups=mesh['mp'=64,'head'=4] {'mp'}, use_global_device_ids=true, to_apply=%region_3.4 | all-reduce | flops 128 | bytes 1024 | tf_op jit(solution)/shard_map/pmax | solution.py:41
  475.7 2.9 fusion.11
  478.6 16.8 %copy.22 = f32[8,16,4096]{0,1,2:T(8,128)} copy(f32[8,16,4096]{2,1,0:T(8,128)S(1)} %fusion.11) | data formatting | bytes 4194304
  495.4 23.7 %reshape.56 = f32[4096,128]{1,0:T(8,128)} reshape(f32[4096,16,8]{2,1,0:T(8,128)} %bitcast.23) | data formatting | bytes 4194304
  519.1 0.0 reduce-scatter.4.cloned.1.call-update
  519.1 0.2 reshape.53
  519.3 0.2 fusion.9
  519.5 126.2 %psum.29 = f32[8,16]{1,0:T(8,128)S(1)} all-reduce(f32[8,16]{1,0:T(8,128)S(1)} %fusion.9), channel_id=1, replica_groups=mesh['mp'=64,'head'=4] {'mp'}, use_global_device_ids=true, to_apply=%region_6.7 | all-reduce | flops 128 | bytes 1024 | tf_op jit(solution)/shard_map/psum | solution.py:43
  645.7 0.1 copy.19
  645.7 8.6 reduce-scatter.4.cloned.1.call-done
  654.4 1.0 reshape.57
  655.4 0.2 copy.23
  655.7 0.2 convolution_bitcast_fusion
  655.9 246.2 %psum.30 = bf16[8,16,64]{2,0,1:T(8,128)(2,1)S(1)} all-reduce(f32[8,16,64]{2,0,1:T(8,128)S(1)} %convolution_bitcast_fusion), channel_id=1, replica_groups=mesh['mp'=64,'head'=4] {'mp'}, use_global_device_ids=true, to_apply=%region_7.8 | all-reduce | flops 8192 | bytes 49152 | tf_op jit(solution)/shard_map/psum | solution.py:58
  902.2 0.1 reshape.54
  902.3 0.1 fusion.25
  902.4 8.5 psum.31
  910.9 0.7 add_convert_fusion
  (15 shorter events, 0.1 us)
Async XLA Ops:
  6.5 2.7 copy-start
  6.5 337.9 %all-gather.2.cloned.1.call-start = ((), (), s32[]{:S(2)}) async-start(), calls=%async_computation.1 | async-start | bytes 8519680 | tf_op jit(solution)/shard_map/all_gather | solution.py:31
  261.1 393.3 %reduce-scatter.4.cloned.1.call-start = ((), (), s32[]{:S(2)}) async-start(), calls=%async_computation.2 | async-start | bytes 2129920
  261.9 89.8 %copy-start.3 = (f32[32,16]{0,1:T(8,128)S(1)}, f32[32,16]{0,1:T(8,128)}, u32[]{:S(2)}) copy-start(f32[32,16]{0,1:T(8,128)} %param.17) | copy-start | bytes 6148
  261.9 89.8 %copy-start.4 = (s32[8,64]{1,0:T(8,128)S(1)}, s32[8,64]{1,0:T(8,128)}, u32[]{:S(2)}) copy-start(s32[8,64]{1,0:T(8,128)} %param.18) | copy-start | bytes 6148
  495.4 23.7 %copy-start.1 = (bf16[64,1024]{1,0:T(8,128)(2,1)S(1)}, bf16[64,1024]{1,0:T(8,128)(2,1)}, u32[]{:S(2)}) copy-start(bf16[64,1024]{1,0:T(8,128)(2,1)} %param.15) | copy-start | bytes 393220
  519.1 383.2 %copy-start.2 = (bf16[1024,64]{0,1:T(8,128)(2,1)S(1)}, bf16[1024,64]{0,1:T(8,128)(2,1)}, u32[]{:S(2)}) copy-start(bf16[1024,64]{0,1:T(8,128)(2,1)} %param.16) | copy-start | bytes 393220
Sparse Core Ops, SparseCore 0:
  261.2 83.1 all-gather.1
  519.2 135.0 reduce-scatter.3

commit v2 on v1

v2 whole, which is shorter than its diff:
```python
import functools

import jax
import jax.numpy as jnp
from jax import lax
from jax.experimental import pallas as pl
from jax.experimental.pallas import tpu as pltpu
from jax.sharding import PartitionSpec as P

EPSILON = 1e-06
NEGATIVE = -1e30
NX = 4
NC = 2
LANES = 128
MESH = pl.DeviceIdType.MESH
F32 = jnp.float32
BF16 = jnp.bfloat16
NT = (((1,), (1,)), ((), ()))


def split3(value):
    first = value.astype(BF16).astype(F32)
    second = (value - first).astype(BF16).astype(F32)
    return first, second, value - first - second


def pack_stats(top, total):
    parts = split3(top) + split3(total)
    lane = lax.broadcasted_iota(jnp.int32, (top.shape[0], LANES), 1) // 16
    out = jnp.zeros((top.shape[0], LANES), F32)
    for k, part in enumerate(parts):
        out = jnp.where(lane == k, part, out)
    return out


def unpack_stats(stats):
    col = [stats[:, 16 * k : 16 * k + 1] for k in range(6)]
    return col[0] + col[1] + col[2], col[3] + col[4] + col[5]


def opened(block, width):
    block = block.astype(F32)
    return (block[:, :width], *unpack_stats(block[:, width:]))


def merged(parts):
    top = functools.reduce(jnp.maximum, [p[1] for p in parts])
    scales = [jnp.exp(p[1] - top) for p in parts]
    data = functools.reduce(jnp.add, [p[0] * s for p, s in zip(parts, scales)])
    total = functools.reduce(jnp.add, [p[2] * s for p, s in zip(parts, scales)])
    return data, top, total


def closed(part):
    data, top, total = part
    return jnp.concatenate([data, pack_stats(top, total)], axis=1).astype(BF16)


def kernel(
    nz,
    ny,
    n_send,
    n_recv,
    table,
    src_len,
    hidden,
    gain,
    w_query,
    enc,
    w_key,
    w_value,
    w_out,
    buckets,
    out,
    hid_v,
    gain_v,
    wq_v,
    wo_v,
    bk_v,
    enc_v,
    kw,
    vw,
    qz,
    qx,
    probe,
    add_v,
    mix,
    sib,
    half,
    hop,
    zsend,
    zrecv,
    cx,
    cz,
    yo,
    local_sem,
    enc_sem,
    send_sem,
    recv_sem,
):
    batch = hid_v.shape[0]
    width = nz * LANES
    me = lax.axis_index("mp")
    my_y = lax.axis_index("head")
    z = me // (NX * NC)
    x = lax.rem(me // NC, NX)
    c = lax.rem(me, NC)
    other = 1 - c

    def mp_of(zz, xx, cc):
        return (zz * NX + xx) * NC + cc

    def zat(dz):
        return lax.rem(z + dz, nz)

    def xat(dx):
        return lax.rem(x + dx, NX)

    far = sorted(range(1, nz), key=lambda d: -min(d, nz - d))
    near = far[::-1]
    sends = []
    counts = {"send": 0, "recv": 0}

    def fresh(kind, number):
        first = counts[kind]
        counts[kind] += number
        return first

    def copy_to(src, dst, recv, device):
        copy = pltpu.make_async_remote_copy(
            src_ref=src,
            dst_ref=dst,
            send_sem=send_sem.at[fresh("send", 1)],
            recv_sem=recv_sem.at[recv],
            device_id=device,
            device_id_type=MESH,
        )
        copy.start()
        sends.append(copy)

    def landed(dst, recv):
        pltpu.make_async_remote_copy(
            src_ref=dst,
            dst_ref=dst,
            send_sem=send_sem.at[0],
            recv_sem=recv_sem.at[recv],
            device_id={"mp": me},
            device_id_type=MESH,
        ).wait_recv()

    def mp(zz, xx, cc):
        return {"mp": mp_of(zz, xx, cc)}

    barrier = pltpu.get_barrier_semaphore()
    peers = [mp(z, xat(dx), cc) for dx in range(1, NX) for cc in (0, 1)]
    peers += [mp(z, x, other)]
    peers += [mp(zat(dz), x, cc) for dz in far for cc in (0, 1)]
    peers += [{"head": lax.rem(my_y + dy, ny)} for dy in range(1, ny)]
    for peer in peers:
        pl.semaphore_signal(barrier, inc=1, device_id=peer, device_id_type=MESH)

    local = [
        pltpu.make_async_copy(src, dst, local_sem.at[k])
        for k, (src, dst) in enumerate(
            [
                (hidden, hid_v),
                (w_query, wq_v),
                (gain, gain_v),
                (buckets, bk_v),
                (w_out, wo_v),
                (w_key.at[:, pl.ds(pl.multiple_of(z * LANES, LANES), LANES)], kw.at[z, c]),
                (w_value.at[:, pl.ds(pl.multiple_of(z * LANES, LANES), LANES)], vw.at[z, c]),
            ]
        )
    ]
    for copy in local:
        copy.start()
    for xx in range(NX):
        for zz in range(nz):
            pltpu.make_async_copy(
                enc.at[:, pl.ds(zz * NX * LANES + xx * LANES, LANES)],
                enc_v.at[xx, :, pl.ds(zz * LANES, LANES)],
                enc_sem.at[xx],
            ).start()

    local[0].wait()
    wide = hid_v[...].astype(F32)
    mean_square = jnp.mean(wide * wide, axis=-1, keepdims=True)
    local[2].wait()
    lanes_of = pl.ds(pl.multiple_of((z * NX + x) * LANES, LANES), LANES)
    block = hid_v[:, lanes_of].astype(F32) * lax.rsqrt(mean_square + EPSILON) * gain_v[:, lanes_of]
    block = jnp.where(c == 1, pltpu.roll(block, LANES // 2, 1), block)
    local[1].wait()
    query = jnp.dot(
        block[:, : LANES // 2].astype(BF16), wq_v[...], preferred_element_type=F32
    )
    own_q = qz.at[0]
    stage = qz.at[1]
    for zz in range(nz):
        stage[zz] = query[:, zz * LANES : (zz + 1) * LANES]
    own_q[z] = stage[z]
    pl.semaphore_wait(barrier, len(peers))
    base = fresh("recv", nz)
    for dz in far:
        copy_to(stage.at[zat(dz)], own_q.at[z], base + z, mp(zat(dz), x, c))
    key_base = fresh("recv", nz)
    for dz in far:
        cols = pl.ds(pl.multiple_of(zat(dz) * LANES, LANES), LANES)
        copy_to(w_key.at[:, cols], kw.at[z, c], key_base + z, mp(zat(dz), x, c))
    value_base = fresh("recv", nz)
    for dz in far:
        cols = pl.ds(pl.multiple_of(zat(dz) * LANES, LANES), LANES)
        copy_to(w_value.at[:, cols], vw.at[z, c], value_base + z, mp(zat(dz), x, c))

    local[3].wait()
    table_rows = batch
    ids = jnp.concatenate([bk_v[...], bk_v[...]], axis=1)
    row_b = lax.broadcasted_iota(jnp.int32, (batch, LANES), 0)
    lane = lax.broadcasted_iota(jnp.int32, (batch, LANES), 1)
    lens = jnp.zeros((batch, LANES), jnp.int32)
    for b in range(batch):
        lens = jnp.where(row_b == b, src_len[b], lens)
    per = LANES // 2
    position = me * per + lax.rem(lane, per)
    live = (position < lens) & (lane // per == lax.rem(row_b, 2))

    def add_bucket(k, rows):
        hit = ids == k
        return tuple(
            jnp.where(hit, table[h, k], row) for h, row in enumerate(rows)
        )

    rows = lax.fori_loop(
        0,
        table.shape[1],
        add_bucket,
        tuple(jnp.zeros((batch, LANES), F32) for _ in range(NC * nz)),
    )
    for cc in range(NC):
        for zz in range(nz):
            add_v[pl.ds((cc * nz + zz) * batch, batch), :] = rows[NC * zz + cc]

    for dz in near[::-1]:
        landed(own_q.at[zat(dz)], base + zat(dz))
    pair = functools.reduce(jnp.add, [own_q[zz] for zz in range(nz)])
    qx[x, c] = pair
    base = fresh("recv", NX * NC)
    for dx in (2, 1, 3, 0):
        for cc in range(NC):
            peer_c = lax.rem(c + cc, NC)
            if dx or cc:
                copy_to(qx.at[x, c], qx.at[x, c], base + x * NC + c, mp(z, xat(dx), peer_c))

    local[5].wait()
    for dz in far:
        landed(kw.at[zat(dz), c], key_base + zat(dz))
    sib_base = fresh("recv", 2)
    copy_to(kw.at[:, c], kw.at[:, c], sib_base, mp(z, x, other))

    for dx in range(NX):
        for cc in range(NC):
            peer_c = lax.rem(c + cc, NC)
            if dx or cc:
                landed(qx.at[xat(dx), peer_c], base + xat(dx) * NC + peer_c)
    pair = functools.reduce(
        jnp.add, [qx[xx, cc] for xx in range(NX) for cc in range(NC)]
    ).astype(BF16).astype(F32)
    pair = jnp.where(lane // per == c, pair * (float(per) ** -0.5), 0.0).astype(BF16)
    landed(kw.at[:, other], sib_base)
    mine = lax.dot_general(
        pair, kw[...].reshape(width, LANES), NT, preferred_element_type=F32
    )
    probe[x, c, z] = mine.astype(BF16)

    z_base = fresh("recv", nz)
    for dz in far:
        copy_to(probe.at[x, c, z], probe.at[x, c, z], z_base + z, mp(zat(dz), x, c))
    right_base = fresh("recv", nz)
    left_base = fresh("recv", nz)
    fwd_base = fresh("recv", nz)
    core_base = fresh("recv", NX)
    order = [0] + near

    def along_x(dz):
        zz = zat(dz)
        copy_to(probe.at[x, c, zz], probe.at[x, c, zz], right_base + zz, mp(zz * 0 + z, xat(1), c))
        copy_to(probe.at[x, c, zz], probe.at[x, c, zz], left_base + zz, mp(zz * 0 + z, xat(3), c))

    def relay(n, dz):
        zz = zat(dz)
        if n % 2 == 0:
            landed(probe.at[xat(3), c, zz], right_base + zz)
            copy_to(probe.at[xat(3), c, zz], probe.at[xat(3), c, zz], fwd_base + zz, mp(z, xat(1), c))
        else:
            landed(probe.at[xat(1), c, zz], left_base + zz)
            copy_to(probe.at[xat(1), c, zz], probe.at[xat(1), c, zz], fwd_base + zz, mp(z, xat(3), c))

    along_x(0)
    for n, dz in enumerate(order[1:]):
        landed(probe.at[x, c, zat(dz)], z_base + zat(dz))
        along_x(dz)
    copy_to(probe.at[x, c], probe.at[x, c], core_base + x, mp(z, x, other))
    for n, dz in enumerate(order):
        relay(n, dz)
    for n, dz in enumerate(order):
        zz = zat(dz)
        if n % 2 == 0:
            landed(probe.at[xat(1), c, zz], left_base + zz)
        else:
            landed(probe.at[xat(3), c, zz], right_base + zz)
    for dx in (1, 3):
        copy_to(probe.at[xat(dx), c], probe.at[xat(dx), c], core_base + xat(dx), mp(z, xat(0), other))

    def columns_in(xx):
        pltpu.make_async_copy(enc_v.at[xx], enc_v.at[xx], enc_sem.at[xx]).wait()

    for xx in range(NX):
        columns_in(xx)

    def score_part(xx):
        rows_in = jnp.concatenate(
            [probe[xx, cc, zz].astype(F32) for cc in range(NC) for zz in range(nz)], axis=0
        ).astype(BF16)
        return lax.dot_general(rows_in, enc_v[xx], NT, preferred_element_type=F32)

    landed(probe.at[x, other], core_base + x)
    scores = score_part(x)
    for n, dz in enumerate(order):
        zz = zat(dz)
        landed(probe.at[xat(2), c, zz], fwd_base + zz)
    copy_to(probe.at[xat(2), c], probe.at[xat(2), c], core_base + xat(2), mp(z, x, other))
    for dx in (1, 3, 2):
        landed(probe.at[xat(dx), other], core_base + xat(dx))
        scores = scores + score_part(xat(dx))

    heads = NC * nz
    n_rows = heads * batch
    blocks = scores.shape[1] // LANES
    row_all = lax.rem(lax.broadcasted_iota(jnp.int32, (n_rows, LANES), 0), batch)
    picked = jnp.zeros((n_rows, LANES), F32)
    for k in range(blocks):
        picked = jnp.where(row_all // 2 == k, scores[:, k * LANES : (k + 1) * LANES], picked)
    alive = jnp.concatenate([live.astype(F32)] * heads, axis=0) > 0.5
    picked = jnp.where(alive, picked + add_v[...], NEGATIVE)
    top = jnp.max(picked, axis=1, keepdims=True)
    weights = jnp.where(alive, jnp.exp(picked - top), 0.0).astype(BF16).astype(F32)
    total = jnp.sum(weights, axis=1, keepdims=True)
    spread = jnp.concatenate(
        [jnp.where(row_all // 2 == k, weights, 0.0) for k in range(blocks)], axis=1
    ).astype(BF16)
    stats = pack_stats(top, total).astype(BF16)
    per_core = nz * batch

    core_base = fresh("recv", NX)
    for dx in (2, 1, 3, 0):
        xx = xat(dx)
        mixed = jnp.dot(spread, enc_v[xx], preferred_element_type=F32).astype(BF16)
        for cc in range(NC):
            mix[cc, xx, :, pl.ds(0, width)] = mixed[cc * per_core : (cc + 1) * per_core]
            mix[cc, xx, :, pl.ds(width, LANES)] = stats[cc * per_core : (cc + 1) * per_core]
        copy_to(mix.at[other, xx], sib.at[xx], core_base + xx, mp(z, x, other))

    def both_cores(xx):
        landed(sib.at[xx], core_base + xx)
        return merged([opened(mix[c, xx], width), opened(sib[xx], width)])

    mid = per_core // 2
    half_base = fresh("recv", 2)
    hop_base = fresh("recv", 4)
    far_part = closed(both_cores(xat(2)))
    half[0, 0] = far_part[:mid]
    half[0, 1] = far_part[mid:]
    copy_to(half.at[0, 0], half.at[1, 0], half_base, mp(z, xat(1), c))
    copy_to(half.at[0, 1], half.at[1, 1], half_base + 1, mp(z, xat(3), c))

    right_part = both_cores(xat(1))
    right_low = closed(tuple(p[mid:] for p in right_part))
    hop[0, 0, 1] = right_low
    copy_to(hop.at[0, 0, 1], hop.at[1, 0, 1], hop_base + 1, mp(z, xat(1), c))
    left_part = both_cores(xat(3))
    hop[0, 1, 0] = closed(tuple(p[:mid] for p in left_part))
    copy_to(hop.at[0, 1, 0], hop.at[1, 1, 0], hop_base + 2, mp(z, xat(3), c))

    landed(half.at[1, 0], half_base)
    hop[0, 0, 0] = closed(
        merged([tuple(p[:mid] for p in right_part), opened(half[1, 0], width)])
    )
    copy_to(hop.at[0, 0, 0], hop.at[1, 0, 0], hop_base, mp(z, xat(1), c))
    landed(half.at[1, 1], half_base + 1)
    hop[0, 1, 1] = closed(
        merged([tuple(p[mid:] for p in left_part), opened(half[1, 1], width)])
    )
    copy_to(hop.at[0, 1, 1], hop.at[1, 1, 1], hop_base + 3, mp(z, xat(3), c))

    local[6].wait()
    for dz in far:
        landed(vw.at[zat(dz), c], value_base + zat(dz))
    copy_to(vw.at[:, c], vw.at[:, c], sib_base + 1, mp(z, x, other))

    own = both_cores(xat(0))
    for part, (first, second) in enumerate(((1, 2), (0, 3))):
        pass
    landed(hop.at[1, 0, 1], hop_base + 1)
    landed(hop.at[1, 1, 0], hop_base + 2)
    landed(hop.at[1, 0, 0], hop_base)
    landed(hop.at[1, 1, 1], hop_base + 3)
    for part in range(2):
        rows_of = slice(part * mid, (part + 1) * mid)
        done = merged(
            [
                tuple(p[rows_of] for p in own),
                opened(hop[1, 0, part], width),
                opened(hop[1, 1, part], width),
            ]
        )
        packed = closed(done)
        for k in range(nz // 2):
            zsend[part * (nz // 2) + k] = packed[k * batch : (k + 1) * batch]
    z_base = fresh("recv", nz)
    for dz in far:
        copy_to(zsend.at[zat(dz)], zrecv.at[z], z_base + z, mp(zat(dz), x, c))
    parts = [opened(zsend[z], width)]
    for dz in far:
        landed(zrecv.at[zat(dz)], z_base + zat(dz))
    for dz in far:
        parts.append(opened(zrecv[zat(dz)], width))
    data, _, total = merged(parts)
    mean = (data / total).astype(BF16)

    landed(vw.at[:, other], sib_base + 1)
    context = jnp.dot(mean, vw[...].reshape(width, LANES), preferred_element_type=F32)
    cx[x] = jnp.where(lane // per == c, context, 0.0)
    x_base = fresh("recv", NX)
    for dx in (2, 1, 3):
        copy_to(cx.at[x], cx.at[x], x_base + x, mp(z, xat(dx), c))
    for dx in (1, 3, 2):
        landed(cx.at[xat(dx)], x_base + xat(dx))
    cz[z, c] = functools.reduce(jnp.add, [cx[xx] for xx in range(NX)]).astype(BF16)
    base = fresh("recv", nz * NC)
    for dz in far + [0]:
        for cc in range(NC):
            peer_c = lax.rem(c + cc, NC)
            if dz or cc:
                copy_to(cz.at[z, c], cz.at[z, c], base + z * NC + c, mp(zat(dz), x, peer_c))
    for dz in [0] + near:
        for cc in range(NC):
            peer_c = lax.rem(c + cc, NC)
            if dz or cc:
                landed(cz.at[zat(dz), peer_c], base + zat(dz) * NC + peer_c)
    full = jnp.concatenate(
        [cz[zz, 0].astype(F32) + cz[zz, 1].astype(F32) for zz in range(nz)], axis=1
    ).astype(BF16)
    local[4].wait()
    yo[my_y] = lax.dot_general(full, wo_v[...], NT, preferred_element_type=F32)
    base = fresh("recv", ny)
    for dy in sorted(range(1, ny), key=lambda d: -min(d, ny - d)):
        peer = lax.rem(my_y + dy, ny)
        copy_to(yo.at[my_y], yo.at[my_y], base + my_y, {"head": peer})
    for dy in range(1, ny):
        peer = lax.rem(my_y + dy, ny)
        landed(yo.at[peer], base + peer)
    out[...] = functools.reduce(jnp.add, [yo[k] for k in range(ny)])
    for copy in sends:
        copy.wait_send()
    assert counts["send"] <= n_send and counts["recv"] <= n_recv, counts


def shards(
    nz, ny, hidden, norm_gain, w_query, enc, w_key, w_value, w_out, bias_table, buckets, src_len
):
    batch, src_local, model = enc.shape
    rows, inner = w_key.shape
    cols = w_out.shape[1]
    width = nz * LANES
    per_core = nz * batch
    n_send, n_recv = 128, 192
    me = lax.axis_index("mp")
    any_space = pl.BlockSpec(memory_space=pl.ANY)
    smem = pl.BlockSpec(memory_space=pltpu.SMEM)
    summed = pl.pallas_call(
        functools.partial(kernel, nz, ny, n_send, n_recv),
        out_shape=jax.ShapeDtypeStruct((batch, cols), F32),
        in_specs=[smem, smem] + [any_space] * 8,
        out_specs=pl.BlockSpec(memory_space=pltpu.VMEM),
        scratch_shapes=[
            pltpu.VMEM((batch, model), BF16),
            pltpu.VMEM((1, model), F32),
            pltpu.VMEM((rows, inner), BF16),
            pltpu.VMEM((cols, inner), BF16),
            pltpu.VMEM((batch, src_local), jnp.int32),
            pltpu.VMEM((NX, batch * src_local, width), BF16),
            pltpu.VMEM((nz, NC, rows, LANES), BF16),
            pltpu.VMEM((nz, NC, rows, LANES), BF16),
            pltpu.VMEM((2, nz, batch, LANES), F32),
            pltpu.VMEM((NX, NC, batch, LANES), F32),
            pltpu.VMEM((NX, NC, nz, batch, width), BF16),
            pltpu.VMEM((NC * per_core, LANES), F32),
            pltpu.VMEM((NC, NX, per_core, width + LANES), BF16),
            pltpu.VMEM((NX, per_core, width + LANES), BF16),
            pltpu.VMEM((2, 2, per_core // 2, width + LANES), BF16),
            pltpu.VMEM((2, 2, 2, per_core // 2, width + LANES), BF16),
            pltpu.VMEM((nz, batch, width + LANES), BF16),
            pltpu.VMEM((nz, batch, width + LANES), BF16),
            pltpu.VMEM((NX, batch, LANES), F32),
            pltpu.VMEM((nz, NC, batch, LANES), BF16),
            pltpu.VMEM((ny, batch, cols), F32),
            pltpu.SemaphoreType.DMA((8,)),
            pltpu.SemaphoreType.DMA((NX,)),
            pltpu.SemaphoreType.DMA((n_send,)),
            pltpu.SemaphoreType.DMA((n_recv,)),
        ],
        compiler_params=pltpu.CompilerParams(
            collective_id=0, has_side_effects=True, vmem_limit_bytes=48 * 1024 * 1024
        ),
        name="attend",
    )(
        bias_table.T,
        src_len,
        hidden,
        norm_gain.reshape(1, model),
        w_query,
        enc.reshape(batch * src_local, model),
        w_key,
        w_value,
        w_out.T,
        buckets,
    )
    residual = lax.dynamic_slice_in_dim(hidden, me * cols, cols, 1).astype(F32)
    return (summed + residual).astype(BF16)


def solution(mesh):
    ny = mesh.shape["head"]
    nz = mesh.shape["mp"] // (NX * NC)
    in_specs = (
        P(),
        P(),
        P("mp", "head"),
        P(None, "mp", None),
        P("mp", "head"),
        P("mp", "head"),
        P("head", "mp"),
        P(None, "head"),
        P(None, "mp"),
        P(),
    )
    return jax.shard_map(
        functools.partial(shards, nz, ny),
        mesh=mesh,
        in_specs=in_specs,
        out_specs=P(None, "mp"),
        check_vma=False,
    )
```

time: 924 us -> 75.1 us (0.08)
  blocking collectives: 754 us -> 0 us
  waiting for transfers between devices: 91.2 us -> 0 us
  Pallas kernels: 0 us -> 64.6 us
  local copies, waits for them, and re-layouts: 45 us -> 9.4 us
  between operations: 13.5 us -> 0.02 us
  matrix products: 11.3 us -> 0 us
    psum x4 -> x0, blocking collectives: 630 us -> none  [the longest x1 249 us: shards(): lax.psum(query, 'mp').astype(jnp.bfloat16).reshape(batch, heads, head_size)]
    pmax x1 -> x0, blocking collectives: 124 us -> none  [shards(): top = lax.pmax(jnp.max(scores, axis=-1), 'mp')]
    all_gather x1 -> x0, waiting for transfers between devices: 82.5 us -> none  [shards(): probe = lax.all_gather(probe, 'mp', axis=2, tiled=True)]
    pallas_call x0 -> x1, Pallas kernels: none -> 64.6 us  [shards(): pl.pallas_call(functools.partial(kernel, nz, ny, n_send, n_recv), out_sha...]
    unnamed x14 -> x20, local copies, waits for them, and re-layouts: 41.8 us -> 9.4 us
    dot_general x7 -> x0, matrix products: 11.3 us -> none  [the longest x1 7.29 us: shards(): jnp.einsum('bhd,bsd->bhs', probe, enc_states, preferred_element_type=jnp....]
  transfers between devices with their start and end apart: 2 -> 0, of which waited for: 2 -> 0; matrix products, arithmetic and copies ran while one was open for 0% -> 0% of each run, Pallas kernels for 0% -> 0%
where the time goes in v2:
time: 75.1 us; the launch traced here: 74.7 us
  Pallas kernels  64.6 us (86%)
  local copies, waits for them, and re-layouts  9.4 us (13%)
    pallas_call x1, Pallas kernels, shards(): pl.pallas_call(functools.partial(kernel, nz, ny, n_send, n_recv), out_sha...  64.6 us
    unnamed x20, local copies, waits for them, and re-layouts  9.4 us

profile of v2, /device:TPU:1, one launch (start us, length us, event | category | flops | bytes accessed | tf_op | source)
XLA Modules:
  0.0 74.7 jit_solution(16836882867379342003)
XLA Ops:
  0.0 0.0 copy-start
  0.0 2.2 %copy-done = bf16[8,64,4096]{2,1,0:T(8,128)(2,1)S(1)} copy-done((bf16[8,64,4096]{2,1,0:T(8,128)(2,1)S(1)}, bf16[8,64,4096]{2,1,0:T(8,128)(2,1)}, u32[]{:S(2)}) %copy-start) | copy-done | bytes 4194328
  2.2 0.0 copy-start.1
  2.2 0.9 %copy-done.1 = bf16[64,1024]{1,0:T(8,128)(2,1)S(1)} copy-done((bf16[64,1024]{1,0:T(8,128)(2,1)S(1)}, bf16[64,1024]{1,0:T(8,128)(2,1)}, u32[]{:S(2)}) %copy-start.1) | copy-done | bytes 131096
  3.1 0.0 copy-start.2
  3.1 0.9 %copy-done.2 = bf16[64,1024]{1,0:T(8,128)(2,1)S(1)} copy-done((bf16[64,1024]{1,0:T(8,128)(2,1)S(1)}, bf16[64,1024]{1,0:T(8,128)(2,1)}, u32[]{:S(2)}) %copy-start.2) | copy-done | bytes 131096
  4.0 0.0 copy-start.3
  4.0 0.9 %copy-done.3 = bf16[64,1024]{1,0:T(8,128)(2,1)S(1)} copy-done((bf16[64,1024]{1,0:T(8,128)(2,1)S(1)}, bf16[64,1024]{1,0:T(8,128)(2,1)}, u32[]{:S(2)}) %copy-start.3) | copy-done | bytes 131096
  4.9 0.0 copy-start.4
  4.9 0.9 %copy-done.4 = bf16[1024,64]{0,1:T(8,128)(2,1)S(1)} copy-done((bf16[1024,64]{0,1:T(8,128)(2,1)S(1)}, bf16[1024,64]{0,1:T(8,128)(2,1)}, u32[]{:S(2)}) %copy-start.4) | copy-done | bytes 131096
  5.8 0.0 copy-start.5
  5.8 0.8 %copy-done.5 = bf16[8,4096]{1,0:T(8,128)(2,1)S(1)} copy-done((bf16[8,4096]{1,0:T(8,128)(2,1)S(1)}, bf16[8,4096]{1,0:T(8,128)(2,1)}, u32[]{:S(2)}) %copy-start.5) | copy-done | bytes 65560
  6.6 0.0 copy-start.6
  6.7 0.7 copy-done.6
  7.4 0.0 copy-start.7
  7.4 0.7 copy-done.7
  8.1 0.0 copy-start.8
  8.1 0.7 copy-done.8
  8.8 0.0 copy-start.9
  8.8 0.7 copy-done.9
  9.4 64.6 %attend.1 = f32[8,64]{1,0:T(8,128)S(1)} custom-call(f32[16,32]{1,0:T(8,128)S(1)} %bitcast.7, s32[8]{0:T(128)S(1)} %copy-done.9, bf16[8,4096]{1,0:T(8,128)(2,1)S(1)} %copy-done.5, f32[1,4096]{1,0:T(1,128)S(1)} %bitcast.6, bf16[64,1024]{1,0:T(8,128)(2,1)S(1)} %copy-done.1, bf16[512,4096]{1,0:T(8,128)(2,1)S(1)} %bitcast.4, bf16[64,1024]{1,0:T(8,128)(2,1)S(1)} %copy-done.2, ...), custom_call_target="tpu_custom_call" | custom-call | tf_op jit(solution)/shard_map/attend/pallas_call | solution.py:480
  74.0 0.7 add_convert_fusion
Async XLA Ops:
  0.0 2.2 %copy-start = (bf16[8,64,4096]{2,1,0:T(8,128)(2,1)S(1)}, bf16[8,64,4096]{2,1,0:T(8,128)(2,1)}, u32[]{:S(2)}) copy-start(bf16[8,64,4096]{2,1,0:T(8,128)(2,1)} %param.13) | copy-start | bytes 12582916
  2.2 0.9 %copy-start.1 = (bf16[64,1024]{1,0:T(8,128)(2,1)S(1)}, bf16[64,1024]{1,0:T(8,128)(2,1)}, u32[]{:S(2)}) copy-start(bf16[64,1024]{1,0:T(8,128)(2,1)} %w_query.1) | copy-start | bytes 393220
  3.1 0.9 %copy-start.2 = (bf16[64,1024]{1,0:T(8,128)(2,1)S(1)}, bf16[64,1024]{1,0:T(8,128)(2,1)}, u32[]{:S(2)}) copy-start(bf16[64,1024]{1,0:T(8,128)(2,1)} %w_key.1) | copy-start | bytes 393220
  4.0 0.9 %copy-start.3 = (bf16[64,1024]{1,0:T(8,128)(2,1)S(1)}, bf16[64,1024]{1,0:T(8,128)(2,1)}, u32[]{:S(2)}) copy-start(bf16[64,1024]{1,0:T(8,128)(2,1)} %w_value.1) | copy-start | bytes 393220
  4.9 0.9 %copy-start.4 = (bf16[1024,64]{0,1:T(8,128)(2,1)S(1)}, bf16[1024,64]{0,1:T(8,128)(2,1)}, u32[]{:S(2)}) copy-start(bf16[1024,64]{0,1:T(8,128)(2,1)} %param.16) | copy-start | bytes 393220
  5.8 0.8 %copy-start.5 = (bf16[8,4096]{1,0:T(8,128)(2,1)S(1)}, bf16[8,4096]{1,0:T(8,128)(2,1)}, u32[]{:S(2)}) copy-start(bf16[8,4096]{1,0:T(8,128)(2,1)} %hidden.1) | copy-start | bytes 196612
  6.6 0.7 copy-start.6
  7.4 0.7 copy-start.7
  8.1 0.7 copy-start.8
  8.8 0.7 copy-start.9

commit v3 on v2

v3 whole, which is shorter than its diff:
```python
import functools

import jax
import jax.numpy as jnp
from jax import lax
from jax.experimental import pallas as pl
from jax.experimental.pallas import tpu as pltpu
from jax.sharding import PartitionSpec as P

EPSILON = 1e-06
NEGATIVE = -1e30
NX = 4
NC = 2
LANES = 128
MESH = pl.DeviceIdType.MESH
F32 = jnp.float32
BF16 = jnp.bfloat16
NT = (((1,), (1,)), ((), ()))


def split3(value):
    first = value.astype(BF16).astype(F32)
    second = (value - first).astype(BF16).astype(F32)
    return first, second, value - first - second


def pack_stats(top, total):
    parts = split3(top) + split3(total)
    lane = lax.broadcasted_iota(jnp.int32, (top.shape[0], LANES), 1) // 16
    out = jnp.zeros((top.shape[0], LANES), F32)
    for k, part in enumerate(parts):
        out = jnp.where(lane == k, part, out)
    return out


def unpack_stats(stats):
    col = [stats[:, 16 * k : 16 * k + 1] for k in range(6)]
    return col[0] + col[1] + col[2], col[3] + col[4] + col[5]


def opened(block, width):
    block = block.astype(F32)
    return (block[:, :width], *unpack_stats(block[:, width:]))


def merged(parts):
    top = functools.reduce(jnp.maximum, [p[1] for p in parts])
    scales = [jnp.exp(p[1] - top) for p in parts]
    data = functools.reduce(jnp.add, [p[0] * s for p, s in zip(parts, scales)])
    total = functools.reduce(jnp.add, [p[2] * s for p, s in zip(parts, scales)])
    return data, top, total


def closed(part):
    data, top, total = part
    return jnp.concatenate([data, pack_stats(top, total)], axis=1).astype(BF16)


def kernel(
    nz,
    ny,
    n_send,
    n_recv,
    table_in,
    len_in,
    hidden,
    gain,
    w_query,
    enc,
    w_key,
    w_value,
    w_out,
    buckets,
    out,
    table,
    src_len,
    hid_v,
    gain_v,
    wq_v,
    wo_v,
    bk_v,
    enc_v,
    kw,
    vw,
    q_stage,
    qz,
    qx,
    probe,
    add_v,
    mix,
    sib,
    half,
    hop,
    zsend,
    zrecv,
    cx,
    cz,
    yo,
    local_sem,
    enc_sem,
    send_sem,
    recv_sem,
):
    batch = hid_v.shape[0]
    width = nz * LANES
    me = lax.axis_index("mp")
    my_y = lax.axis_index("head")
    z = me // (NX * NC)
    x = lax.rem(me // NC, NX)
    c = lax.rem(me, NC)
    other = 1 - c

    def mp(zz, xx, cc):
        return {"mp": (zz * NX + xx) * NC + cc}

    def zat(dz):
        return lax.rem(z + dz, nz)

    def xat(dx):
        return lax.rem(x + dx, NX)

    def piece(xx, cc, zz):
        return (xx * NC + cc) * nz + zz

    far = sorted(range(1, nz), key=lambda d: -min(d, nz - d))
    near = far[::-1]
    counts = {"send": 0, "recv": 0}
    sent = []

    def fresh(kind, number=1):
        first = counts[kind]
        counts[kind] += number
        return first

    def describe(src, dst, send, recv, device):
        return pltpu.make_async_remote_copy(
            src_ref=src,
            dst_ref=dst,
            send_sem=send_sem.at[send],
            recv_sem=recv_sem.at[recv],
            device_id=device,
            device_id_type=MESH,
        )

    def copy_to(src, dst, send, recv, device):
        describe(src, dst, send, recv, device).start()

    def landed(dst, recv):
        describe(dst, dst, 0, recv, {"mp": me}).wait_recv()

    def sending(whole):
        number = fresh("send")
        sent.append((whole, number))
        return number

    first = [(hidden, hid_v), (w_query, wq_v), (gain, gain_v)]
    cols = pl.ds(pl.multiple_of(z * LANES, LANES), LANES)
    later = [
        (w_key.at[:, cols], kw.at[z, c]),
        (w_value.at[:, cols], vw.at[z, c]),
        (buckets, bk_v),
        (table_in, table),
        (len_in, src_len),
        (w_out, wo_v),
    ]
    local = [
        pltpu.make_async_copy(src, dst, local_sem.at[k]) for k, (src, dst) in enumerate(first + later)
    ]
    for copy in local[:3]:
        copy.start()

    barrier = pltpu.get_barrier_semaphore()
    peers = [mp(zat(dz), x, cc) for dz in far for cc in (0, 1)]
    peers += [mp(z, xat(dx), cc) for dx in range(1, NX) for cc in (0, 1)]
    peers += [mp(z, x, other)]
    peers += [{"head": lax.rem(my_y + dy, ny)} for dy in range(1, ny)]
    for peer in peers:
        pl.semaphore_signal(barrier, inc=1, device_id=peer, device_id_type=MESH)

    local[0].wait()
    wide = hid_v[...].astype(F32)
    mean_square = jnp.mean(wide * wide, axis=-1, keepdims=True)
    local[2].wait()
    lanes_of = pl.ds(pl.multiple_of((z * NX + x) * LANES, LANES), LANES)
    block = hid_v[:, lanes_of].astype(F32) * lax.rsqrt(mean_square + EPSILON) * gain_v[:, lanes_of]
    block = jnp.where(c == 1, pltpu.roll(block, LANES // 2, 1), block)
    local[1].wait()
    query = jnp.dot(block[:, : LANES // 2].astype(BF16), wq_v[...], preferred_element_type=F32)
    for zz in range(nz):
        q_stage[zz] = query[:, zz * LANES : (zz + 1) * LANES]
    qz[z] = q_stage[z]
    pl.semaphore_wait(barrier, len(peers))
    send, qz_recv = sending(q_stage.at[pl.ds(0, nz - 1)]), fresh("recv")
    for dz in far:
        copy_to(q_stage.at[zat(dz)], qz.at[z], send, qz_recv, mp(zat(dz), x, c))
    blocks_recv = []
    for source, target in ((w_key, kw), (w_value, vw)):
        send, recv = sending(target.at[pl.ds(0, nz - 1), 0]), fresh("recv")
        blocks_recv.append(recv)
        for dz in far:
            cols = pl.ds(pl.multiple_of(zat(dz) * LANES, LANES), LANES)
            copy_to(source.at[:, cols], target.at[z, c], send, recv, mp(zat(dz), x, c))
    for copy in local[3:]:
        copy.start()
    for xx in range(NX):
        for zz in range(nz):
            pltpu.make_async_copy(
                enc.at[:, pl.ds((zz * NX + xx) * LANES, LANES)],
                enc_v.at[xx, :, pl.ds(zz * LANES, LANES)],
                enc_sem.at[xx],
            ).start()

    for copy in local[5:8]:
        copy.wait()
    ids = jnp.concatenate([bk_v[...], bk_v[...]], axis=1)
    row_b = lax.broadcasted_iota(jnp.int32, (batch, LANES), 0)
    lane = lax.broadcasted_iota(jnp.int32, (batch, LANES), 1)
    lens = jnp.zeros((batch, LANES), jnp.int32)
    for b in range(batch):
        lens = jnp.where(row_b == b, src_len[b], lens)
    per = LANES // 2
    position = me * per + lax.rem(lane, per)
    live = (position < lens) & (lane // per == lax.rem(row_b, 2))

    def add_bucket(k, rows):
        hit = ids == k
        return tuple(jnp.where(hit, table[h, k], row) for h, row in enumerate(rows))

    rows = lax.fori_loop(
        0,
        table.shape[1],
        add_bucket,
        tuple(jnp.zeros((batch, LANES), F32) for _ in range(NC * nz)),
    )
    for cc in range(NC):
        for zz in range(nz):
            add_v[pl.ds((cc * nz + zz) * batch, batch), :] = rows[NC * zz + cc]

    landed(qz.at[pl.ds(0, nz - 1)], qz_recv)
    qx[x * NC + c] = functools.reduce(jnp.add, [qz[zz] for zz in range(nz)])
    n_plane = NX * NC
    send, recv = sending(qx.at[pl.ds(0, n_plane - 1)]), fresh("recv")
    for dx in (2, 1, 3, 0):
        for dc in range(NC):
            if dx or dc:
                copy_to(
                    qx.at[x * NC + c],
                    qx.at[x * NC + c],
                    send,
                    recv,
                    mp(z, xat(dx), lax.rem(c + dc, NC)),
                )
    local[3].wait()
    landed(kw.at[pl.ds(0, nz - 1), c], blocks_recv[0])
    key_sib = fresh("recv")
    copy_to(kw.at[:, c], kw.at[:, c], sending(kw.at[:, c]), key_sib, mp(z, x, other))
    landed(qx.at[pl.ds(0, n_plane - 1)], recv)
    pair = functools.reduce(jnp.add, [qx[k] for k in range(n_plane)]).astype(BF16).astype(F32)
    pair = jnp.where(lane // per == c, pair * (float(per) ** -0.5), 0.0).astype(BF16)
    landed(kw.at[:, other], key_sib)
    mine = lax.dot_general(pair, kw[...].reshape(width, LANES), NT, preferred_element_type=F32)
    probe[piece(x, c, z)] = mine.astype(BF16)

    total_pieces = (nz - 1) + 2 * nz + nz + NX * nz
    send = sending(probe.at[pl.ds(0, total_pieces)])
    z_recv, right_recv, left_recv = fresh("recv", nz), fresh("recv", nz), fresh("recv", nz)
    relay_recv, core_recv = fresh("recv", nz), fresh("recv", NX)
    order = [0] + near

    def pass_on(xx, zz, recv, device):
        spot = probe.at[piece(xx, c, zz)]
        copy_to(spot, spot, send, recv, device)

    def on_z(n, dz):
        zz = zat(dz)
        if dz:
            landed(probe.at[piece(x, c, zz)], z_recv + zz)
        pass_on(x, zz, right_recv + zz, mp(z, xat(1), c))
        pass_on(x, zz, left_recv + zz, mp(z, xat(3), c))
        pass_on(x, zz, core_recv + x, mp(z, x, other))

    def on_x(n, dz):
        zz = zat(dz)
        for dx, recv, back, here in ((3, right_recv, 1, n % 2 == 0), (1, left_recv, 3, n % 2 == 1)):
            landed(probe.at[piece(xat(dx), c, zz)], recv + zz)
            if here:
                pass_on(xat(dx), zz, relay_recv + zz, mp(z, xat(back), c))
            pass_on(xat(dx), zz, core_recv + xat(dx), mp(z, x, other))

    def on_relay(n, dz):
        zz = zat(dz)
        landed(probe.at[piece(xat(2), c, zz)], relay_recv + zz)
        pass_on(xat(2), zz, core_recv + xat(2), mp(z, x, other))

    def score_part(xx):
        landed(probe.at[pl.ds(piece(xx, other, 0), nz)], core_recv + xx)
        rows_in = jnp.concatenate(
            [probe[piece(xx, cc, zz)].astype(F32) for cc in range(NC) for zz in range(nz)], axis=0
        ).astype(BF16)
        return lax.dot_general(rows_in, enc_v[xx], NT, preferred_element_type=F32)

    for dz in near:
        pass_on(x, z, z_recv + z, mp(zat(dz), x, c))
    lag = 5
    for n in range(nz + lag):
        if n < nz:
            on_z(n, order[n])
        if n >= lag:
            on_x(n - lag, order[n - lag])
    for xx in range(NX):
        pltpu.make_async_copy(enc_v.at[xx], enc_v.at[xx], enc_sem.at[xx]).wait()
    scores = score_part(x)
    for n, dz in enumerate(order[:-2]):
        on_relay(n, dz)
    for dx in (1, 3):
        scores = scores + score_part(xat(dx))
    for n, dz in list(enumerate(order))[-2:]:
        on_relay(n, dz)
    scores = scores + score_part(xat(2))

    heads = NC * nz
    n_rows = heads * batch
    blocks = scores.shape[1] // LANES
    row_all = lax.rem(lax.broadcasted_iota(jnp.int32, (n_rows, LANES), 0), batch)
    picked = jnp.zeros((n_rows, LANES), F32)
    for k in range(blocks):
        picked = jnp.where(row_all // 2 == k, scores[:, k * LANES : (k + 1) * LANES], picked)
    alive = jnp.concatenate([live.astype(F32)] * heads, axis=0) > 0.5
    picked = jnp.where(alive, picked + add_v[...], NEGATIVE)
    top = jnp.max(picked, axis=1, keepdims=True)
    weights = jnp.where(alive, jnp.exp(picked - top), 0.0).astype(BF16).astype(F32)
    total = jnp.sum(weights, axis=1, keepdims=True)
    spread = jnp.concatenate(
        [jnp.where(row_all // 2 == k, weights, 0.0) for k in range(blocks)], axis=1
    ).astype(BF16)
    stats = pack_stats(top, total).astype(BF16)
    per_core = nz * batch

    core_recv = fresh("recv", NX)
    mix_send = sending(sib)

    def mix_part(dx):
        xx = xat(dx)
        mixed = jnp.dot(spread, enc_v[xx], preferred_element_type=F32).astype(BF16)
        for cc in range(NC):
            mix[cc, xx, :, pl.ds(0, width)] = mixed[cc * per_core : (cc + 1) * per_core]
            mix[cc, xx, :, pl.ds(width, LANES)] = stats[cc * per_core : (cc + 1) * per_core]
        copy_to(mix.at[other, xx], sib.at[xx], mix_send, core_recv + xx, mp(z, x, other))

    def both_cores(xx):
        landed(sib.at[xx], core_recv + xx)
        return merged([opened(mix[c, xx], width), opened(sib[xx], width)])

    n_group = min(4, nz)
    size = per_core // n_group
    ways = (1, 3)
    split = [range(n_group // 2), range(n_group // 2, n_group)]
    half_send, half_recv = sending(half.at[0]), fresh("recv", n_group)
    hop_send, hop_recv = sending(hop.at[0]), fresh("recv", 2 * n_group)

    def rows_of(part, group):
        return tuple(p[group * size : (group + 1) * size] for p in part)

    def hop_on(way, group, part):
        hop[0, way, group] = closed(part)
        copy_to(
            hop.at[0, way, group],
            hop.at[1, way, group],
            hop_send,
            hop_recv + way * n_group + group,
            mp(z, xat(ways[way]), c),
        )

    def hop_landed(way, group):
        landed(hop.at[1, way, group], hop_recv + way * n_group + group)
        return opened(hop[1, way, group], width)

    mix_part(2)
    mix_part(1)
    mix_part(3)
    landed(sib.at[xat(2)], core_recv + xat(2))
    for way, group in [(w, g) for k in range(n_group // 2) for w, g in ((0, split[0][k]), (1, split[1][k]))]:
        span = pl.ds(group * size, size)
        half[0, group] = closed(
            merged([opened(mix[c, xat(2), span], width), opened(sib[xat(2), span], width)])
        )
        copy_to(
            half.at[0, group],
            half.at[1, group],
            half_send,
            half_recv + group,
            mp(z, xat(ways[way]), c),
        )

    near_parts = []
    for way in range(2):
        near_parts.append(both_cores(xat(ways[way])))
        for group in split[1 - way]:
            hop_on(way, group, rows_of(near_parts[way], group))
    mix_part(0)
    for k in range(n_group // 2):
        for way in range(2):
            group = split[way][k]
            landed(half.at[1, group], half_recv + group)
            hop_on(
                way,
                group,
                merged([rows_of(near_parts[way], group), opened(half[1, group], width)]),
            )
    local[4].wait()
    landed(vw.at[pl.ds(0, nz - 1), c], blocks_recv[1])
    value_sib = fresh("recv")
    copy_to(vw.at[:, c], vw.at[:, c], sending(vw.at[:, c]), value_sib, mp(z, x, other))
    own = both_cores(xat(0))
    z_send, z_recv = sending(zsend.at[pl.ds(0, nz - 1)]), fresh("recv")
    sums = {}
    for way in range(2):
        for group in split[1 - way]:
            sums[group] = merged([rows_of(own, group), hop_landed(way, group)])
    per_group = nz // n_group
    for k in range(n_group // 2):
        for way in range(2):
            group = split[way][k]
            packed = closed(merged([sums[group], hop_landed(way, group)]))
            for m in range(per_group):
                zsend[group * per_group + m] = packed[m * batch : (m + 1) * batch]
    for dz in far:
        copy_to(zsend.at[zat(dz)], zrecv.at[z], z_send, z_recv, mp(zat(dz), x, c))
    parts = [opened(zsend[z], width)]
    landed(zrecv.at[pl.ds(0, nz - 1)], z_recv)
    for dz in far:
        parts.append(opened(zrecv[zat(dz)], width))
    data, _, total = merged(parts)
    mean = (data / total).astype(BF16)

    landed(vw.at[:, other], value_sib)
    context = jnp.dot(mean, vw[...].reshape(width, LANES), preferred_element_type=F32)
    cx[x * NC + c] = jnp.where(lane // per == c, context, 0.0)
    send, recv = sending(cx.at[pl.ds(0, n_plane - 1)]), fresh("recv")
    for dx in (2, 1, 3, 0):
        for dc in range(NC):
            if dx or dc:
                copy_to(
                    cx.at[x * NC + c],
                    cx.at[x * NC + c],
                    send,
                    recv,
                    mp(z, xat(dx), lax.rem(c + dc, NC)),
                )
    landed(cx.at[pl.ds(0, n_plane - 1)], recv)
    cz[z] = functools.reduce(jnp.add, [cx[k] for k in range(n_plane)]).astype(BF16)
    send, recv = sending(cz.at[pl.ds(0, nz - 1)]), fresh("recv")
    for dz in far:
        copy_to(cz.at[z], cz.at[z], send, recv, mp(zat(dz), x, c))
    local[8].wait()
    landed(cz.at[pl.ds(0, nz - 1)], recv)
    full = jnp.concatenate([cz[zz] for zz in range(nz)], axis=1)
    yo[my_y] = lax.dot_general(full, wo_v[...], NT, preferred_element_type=F32)
    if ny > 1:
        send, recv = sending(yo.at[pl.ds(0, ny - 1)]), fresh("recv")
        for dy in sorted(range(1, ny), key=lambda d: -min(d, ny - d)):
            copy_to(yo.at[my_y], yo.at[my_y], send, recv, {"head": lax.rem(my_y + dy, ny)})
        landed(yo.at[pl.ds(0, ny - 1)], recv)
    out[...] = functools.reduce(jnp.add, [yo[k] for k in range(ny)])
    for whole, number in sent:
        describe(whole, whole, number, 0, {"mp": me}).wait_send()
    assert counts["send"] <= n_send and counts["recv"] <= n_recv, counts


def shards(
    nz, ny, hidden, norm_gain, w_query, enc, w_key, w_value, w_out, bias_table, buckets, src_len
):
    batch, src_local, model = enc.shape
    rows, inner = w_key.shape
    cols = w_out.shape[1]
    width = nz * LANES
    per_core = nz * batch
    n_group = min(4, nz)
    n_send, n_recv = 14, 10 + 4 * nz + 2 * NX + 3 * n_group
    me = lax.axis_index("mp")
    any_space = pl.BlockSpec(memory_space=pltpu.HBM)
    summed = pl.pallas_call(
        functools.partial(kernel, nz, ny, n_send, n_recv),
        out_shape=jax.ShapeDtypeStruct((batch, cols), F32),
        in_specs=[any_space] * 10,
        out_specs=pl.BlockSpec(memory_space=pltpu.VMEM),
        scratch_shapes=[
            pltpu.SMEM(bias_table.shape[::-1], F32),
            pltpu.SMEM(src_len.shape, jnp.int32),
            pltpu.VMEM((batch, model), BF16),
            pltpu.VMEM((1, model), F32),
            pltpu.VMEM((rows, inner), BF16),
            pltpu.VMEM((cols, inner), BF16),
            pltpu.VMEM((batch, src_local), jnp.int32),
            pltpu.VMEM((NX, batch * src_local, width), BF16),
            pltpu.VMEM((nz, NC, rows, LANES), BF16),
            pltpu.VMEM((nz, NC, rows, LANES), BF16),
            pltpu.VMEM((nz, batch, LANES), F32),
            pltpu.VMEM((nz, batch, LANES), F32),
            pltpu.VMEM((NX * NC, batch, LANES), F32),
            pltpu.VMEM((NX * NC * nz, batch, width), BF16),
            pltpu.VMEM((NC * per_core, LANES), F32),
            pltpu.VMEM((NC, NX, per_core, width + LANES), BF16),
            pltpu.VMEM((NX, per_core, width + LANES), BF16),
            pltpu.VMEM((2, n_group, per_core // n_group, width + LANES), BF16),
            pltpu.VMEM((2, 2, n_group, per_core // n_group, width + LANES), BF16),
            pltpu.VMEM((nz, batch, width + LANES), BF16),
            pltpu.VMEM((nz, batch, width + LANES), BF16),
            pltpu.VMEM((NX * NC, batch, LANES), F32),
            pltpu.VMEM((nz, batch, LANES), BF16),
            pltpu.VMEM((ny, batch, cols), F32),
            pltpu.SemaphoreType.DMA((9,)),
            pltpu.SemaphoreType.DMA((NX,)),
            pltpu.SemaphoreType.DMA((n_send,)),
            pltpu.SemaphoreType.DMA((n_recv,)),
        ],
        compiler_params=pltpu.CompilerParams(
            collective_id=0, has_side_effects=True, vmem_limit_bytes=67043328
        ),
        name="attend",
    )(
        bias_table.T,
        src_len,
        hidden,
        norm_gain.reshape(1, model),
        w_query,
        enc.reshape(batch * src_local, model),
        w_key,
        w_value,
        w_out.T,
        buckets,
    )
    residual = lax.dynamic_slice_in_dim(hidden, me * cols, cols, 1).astype(F32)
    return (summed + residual).astype(BF16)


def solution(mesh):
    ny = mesh.shape["head"]
    nz = mesh.shape["mp"] // (NX * NC)
    in_specs = (
        P(),
        P(),
        P("mp", "head"),
        P(None, "mp", None),
        P("mp", "head"),
        P("mp", "head"),
        P("head", "mp"),
        P(None, "head"),
        P(None, "mp"),
        P(),
    )
    return jax.shard_map(
        functools.partial(shards, nz, ny),
        mesh=mesh,
        in_specs=in_specs,
        out_specs=P(None, "mp"),
        check_vma=False,
    )
```

time: 75.1 us -> 62.4 us (0.83)
  local copies, waits for them, and re-layouts: 9.4 us -> 0 us
  Pallas kernels: 64.6 us -> 61 us
    unnamed x20 -> x0, local copies, waits for them, and re-layouts: 9.4 us -> none
    pallas_call x1, Pallas kernels: 64.6 us -> 61 us  [shards(): pl.pallas_call(functools.partial(kernel, nz, ny, n_send, n_recv), out_sha...]
where the time goes in v3:
time: 62.4 us; the launch traced here: 62.3 us
  Pallas kernels  61 us (98%)
  other arithmetic  1.34 us (2%)
    pallas_call x1, Pallas kernels, shards(): pl.pallas_call(functools.partial(kernel, nz, ny, n_send, n_recv), out_sha...  61 us
    convert_element_type x1, other arithmetic, shards(): return (summed + residual).astype(BF16)  1.34 us

profile of v3, /device:TPU:1, one launch (start us, length us, event | category | flops | bytes accessed | tf_op | source)
XLA Modules:
  0.0 62.3 jit_solution(11222015967673740879)
XLA Ops:
  0.0 61.0 %attend.1 = f32[8,64]{1,0:T(8,128)} custom-call(f32[16,32]{1,0:T(8,128)} %bitcast.7, s32[8]{0:T(128)} %len_in.1, bf16[8,4096]{1,0:T(8,128)(2,1)} %hidden.1, f32[1,4096]{1,0:T(1,128)} %bitcast.6, bf16[64,1024]{1,0:T(8,128)(2,1)} %w_query.1, bf16[512,4096]{1,0:T(8,128)(2,1)} %bitcast.4, bf16[64,1024]{1,0:T(8,128)(2,1)} %w_key.1, bf16[64,1024]{1,0:T(8,128)(2,1)} %w_value.1, ...), custom_call_target="tpu_custom_call" | custom-call | tf_op jit(solution)/shard_map/attend/pallas_call | solution.py:482
  61.0 1.3 %add_convert_fusion = bf16[8,64]{1,0:T(8,128)(2,1)} fusion(f32[8,64]{1,0:T(8,128)} %attend.1, bf16[8,4096]{1,0:T(8,128)(2,1)} %hidden.1, s32[]{:T(128)S(6)} %select_n.3), kind=kLoop, calls=%fused_computation | loop fusion | flops 1536 | bytes 4100 | tf_op jit(solution)/shard_map/convert_element_type | solution.py:534
